TPU v7x, 32 devices: a whole 2x2x4 slice. The times are simulated.
32 devices in a mesh: seq: 8 (over z, y), batch: 4 (over x, core).
Axes of the slice: x: 2, y: 2, z: 4, core: 2. Of those that a mesh axis runs over, the one named last changes fastest.
Arguments:
- tokens: bfloat16 [4, 8192, 1024], P('batch', 'seq'), may hold values from -6 to 6
- logits: bfloat16 [4, 8192, 256], P('batch', 'seq'), may hold values from -160 to 160
- slot_grad: bfloat16 [4, 256, 1024], P('batch', 'seq'), may hold values from -6 to 6
- phi_param: bfloat16 [1024, 256], P('seq'), may hold values from -0.1875 to 0.1875
Outputs:
- token_grad: bfloat16 [4, 8192, 1024], P('batch', 'seq')
- phi_grad: float32 [1024, 256], P('seq')
All inputs are finite; a program needn't handle non-finite values.
Results may differ from a plain program's by a relative error of at most 0.0049.
Values may be sent and summed in bfloat16 or wider, within the bound.
A program may use at most 64 MiB of HBM per device.

v0:
```python
import jax
import jax.numpy as jnp
from jax import lax
from jax.sharding import PartitionSpec as P


def per_device(tokens, logits, slot_grad, phi_param):
    inputs = tokens[0]
    scores = logits[0].astype(jnp.float32)
    upstream, phi_full = (
        lax.all_gather(slot_grad[0], "seq", axis=0, tiled=True),
        lax.all_gather(phi_param, "seq", axis=0, tiled=True),
    )
    weight_grad = lax.dot_general(
        inputs, upstream, (((1,), (1,)), ((), ())), preferred_element_type=jnp.float32
    )
    col_peak = lax.pmax(jnp.max(scores, axis=0, keepdims=True), "seq")
    raw_weights = jnp.exp(scores - col_peak)
    col_total = lax.psum(jnp.sum(raw_weights, axis=0, keepdims=True), "seq")
    dispatch = raw_weights / col_total
    col_dot = lax.psum(jnp.sum(dispatch * weight_grad, axis=0, keepdims=True), "seq")
    logit_grad = (dispatch * (weight_grad - col_dot)).astype(jnp.bfloat16)
    dispatch_low = dispatch.astype(jnp.bfloat16)
    grad_scale = float(lax.axis_size("seq") * inputs.shape[0] // 16)
    token_sum = jnp.dot(dispatch_low, upstream, preferred_element_type=jnp.float32)
    token_sum = token_sum + lax.dot_general(
        logit_grad, phi_full, (((1,), (1,)), ((), ())), preferred_element_type=jnp.float32
    )
    token_grad = (grad_scale * token_sum).astype(jnp.bfloat16)[None]
    phi_terms = lax.dot_general(
        inputs, logit_grad, (((0,), (0,)), ((), ())), preferred_element_type=jnp.float32
    )
    phi_share = lax.psum_scatter(phi_terms, "seq", scatter_dimension=0, tiled=True)
    phi_grad = lax.psum(phi_share, "batch")
    return (token_grad, phi_grad)


def solution(mesh):
    return jax.shard_map(
        per_device,
        mesh=mesh,
        in_specs=(
            P("batch", "seq", None),
            P("batch", "seq", None),
            P("batch", "seq", None),
            P("seq", None),
        ),
        out_specs=(P("batch", "seq", None), P("seq", None)),
        check_vma=False,
    )
```

profile of v0, /device:TPU:0, one launch (start us, length us, event | category | flops | bytes accessed | tf_op | source)
XLA Modules:
  0.0 210.9 jit_solution(2274995212261977552)
XLA Ops:
  7.2 0.0 copy-start
  7.2 0.0 reduce-scatter.2.cloned.1.call-start
  7.2 1.3 reduce_max.16
  8.6 23.2 %pmax.7 = f32[256]{0:T(256)S(1)} all-reduce(bf16[256]{0:T(256)(128)(2,1)S(1)} %reduce_max.16), channel_id=1, replica_groups=mesh['seq'=8,'batch'=4] {'seq'}, use_global_device_ids=true, to_apply=%region_1.0 | all-reduce | flops 256 | bytes 1536 | tf_op jit(solution)/shard_map/pmax | solution.py:17
  31.7 1.3 fusion.10
  33.0 17.1 %psum.21 = f32[256]{0:T(256)S(1)} all-reduce(f32[256]{0:T(256)S(1)} %fusion.10), channel_id=1, replica_groups=mesh['seq'=8,'batch'=4] {'seq'}, use_global_device_ids=true, to_apply=%region_3.0 | all-reduce | flops 256 | bytes 2048 | tf_op jit(solution)/shard_map/psum | solution.py:19
  50.1 31.5 %all-gather = bf16[1,256,1024]{2,1,0:T(8,128)(2,1)S(1)} all-gather(bf16[1,32,1024]{2,1,0:T(8,128)(2,1)} %param.6), channel_id=2, replica_groups=mesh['seq'=8,'batch'=4] {'seq'}, dimensions={1}, use_global_device_ids=true | all-gather | bytes 589824 | tf_op jit(solution)/shard_map/all_gather | solution.py:11
  81.6 0.0 copy-done
  81.6 0.0 copy-start.2
  81.6 0.0 copy-start.1
  81.6 3.0 %multiply_reduce_fusion = (f32[256]{0:T(256)S(1)}, f32[1024,256]{1,0:T(8,128)}) fusion(f32[256]{0:T(256)S(1)} %psum.21, f32[256]{0:T(256)S(1)} %pmax.7, bf16[1,1024,256]{2,1,0:T(8,128)(2,1)} %param.5, bf16[1,256,1024]{2,1,0:T(8,128)(2,1)S(1)} %all-gather, bf16[1,1024,1024]{2,1,0:T(8,128)(2,1)S(1)} %copy-done), kind=kOutput, calls=%fused_computation.12 | convolution fusion | flops 538181376 | bytes 4197376 | tf_op jit(solution)/shard_map/dot_general | solution.py:14
  84.6 0.0 copy-done.2
  84.6 19.4 %psum.22 = f32[256]{0:T(256)S(1)} all-reduce(f32[256]{0:T(256)S(1)} %get-tuple-element.4), channel_id=1, replica_groups=mesh['seq'=8,'batch'=4] {'seq'}, use_global_device_ids=true, to_apply=%region_5.0 | all-reduce | flops 256 | bytes 2048 | tf_op jit(solution)/shard_map/psum | solution.py:21
  103.9 0.0 copy-done.1
  103.9 0.0 copy-start.3
  103.9 3.0 %fusion.5 = f32[1024,256]{0,1:T(8,128)} fusion(bf16[1,1024,1024]{2,1,0:T(8,128)(2,1)S(1)} %copy-done, f32[1024,256]{1,0:T(8,128)} %get-tuple-element.5, f32[256]{0:T(256)S(1)} %psum.22, f32[256]{0:T(256)S(1)} %psum.21, f32[256]{0:T(256)S(1)} %pmax.7, bf16[1,1024,256]{2,1,0:T(8,128)(2,1)S(1)} %copy-done.1), kind=kOutput, calls=%fused_computation.6 | convolution fusion | flops 538443776 | bytes 4721664 | tf_op jit(solution)/shard_map/dot_general | solution.py:30
  107.0 0.0 reduce-scatter.2.cloned.1.call-update
  107.0 0.0 all-reduce.2.cloned.1.call-start
  107.0 0.0 copy-done.3
  107.0 31.8 %all_gather.7 = bf16[1024,256]{1,0:T(8,128)(2,1)S(1)} all-gather(bf16[128,256]{1,0:T(8,128)(2,1)S(1)} %copy-done.3), channel_id=1, replica_groups=mesh['seq'=8,'batch'=4] {'seq'}, dimensions={0}, use_global_device_ids=true | all-gather | bytes 589824 | tf_op jit(solution)/shard_map/all_gather | solution.py:12
  138.8 3.7 %fusion.12 = f32[1024,1024]{1,0:T(8,128)} fusion(bf16[1,256,1024]{2,1,0:T(8,128)(2,1)} %copy-done.2, bf16[1,1024,256]{2,1,0:T(8,128)(2,1)S(1)} %copy-done.1, f32[256]{0:T(256)S(1)} %psum.21, f32[256]{0:T(256)S(1)} %pmax.7), kind=kOutput, calls=%fused_computation.14 | convolution fusion | flops 537919488 | bytes 5244928 | tf_op jit(solution)/shard_map/dot_general | solution.py:25
  142.5 26.9 %reduce-scatter.2.cloned.1.call-done = f32[128,256]{0,1:T(8,128)} async-done(((f32[1024,256]{0,1:T(8,128)}), f32[128,256]{0,1:T(8,128)}) %reduce-scatter.2.cloned.1.call-update) | async-done | bytes 131088 | tf_op jit(solution)/shard_map/reduce_scatter | solution.py:33
  169.4 0.0 all-reduce.2.cloned.1.call-update
  169.4 4.7 %fusion.4 = bf16[1,1024,1024]{2,1,0:T(8,128)(2,1)} fusion(f32[1024,1024]{1,0:T(8,128)} %fusion.12, bf16[1024,256]{1,0:T(8,128)(2,1)S(1)} %all_gather.7, f32[1024,256]{1,0:T(8,128)} %get-tuple-element.5, f32[256]{0:T(256)S(1)} %psum.22, f32[256]{0:T(256)S(1)} %psum.21, f32[256]{0:T(256)S(1)} %pmax.7, bf16[1,1024,256]{2,1,0:T(8,128)(2,1)S(1)} %copy-done.1), kind=kOutput, calls=%fused_computation.5 | convolution fusion | flops 541589504 | bytes 8391680 | tf_op jit(solution)/shard_map/dot_general | solution.py:26
  174.1 28.3 %all-reduce.2.cloned.1.call-done = f32[128,256]{0,1:T(8,128)} async-done(((f32[128,256]{0,1:T(8,128)}), f32[128,256]{0,1:T(8,128)}) %all-reduce.2.cloned.1.call-update) | async-done | bytes 131088 | tf_op jit(solution)/shard_map/psum | solution.py:34
  202.4 1.7 copy.6
Async XLA Ops:
  7.2 74.4 %copy-start = (bf16[1,1024,1024]{2,1,0:T(8,128)(2,1)S(1)}, bf16[1,1024,1024]{2,1,0:T(8,128)(2,1)}, u32[]{:S(2)}) copy-start(bf16[1,1024,1024]{2,1,0:T(8,128)(2,1)} %param.4) | copy-start | bytes 6291460
  7.2 162.2 %reduce-scatter.2.cloned.1.call-start = ((), (), s32[]{:S(2)}) async-start(), calls=%async_computation.1 | async-start | bytes 1179648 | tf_op jit(solution)/shard_map/reduce_scatter | solution.py:33
  81.6 3.0 %copy-start.2 = (bf16[1,256,1024]{2,1,0:T(8,128)(2,1)}, bf16[1,256,1024]{2,1,0:T(8,128)(2,1)S(1)}, u32[]{:S(2)}) copy-start(bf16[1,256,1024]{2,1,0:T(8,128)(2,1)S(1)} %all-gather) | copy-start | bytes 1572868
  81.6 22.3 %copy-start.1 = (bf16[1,1024,256]{2,1,0:T(8,128)(2,1)S(1)}, bf16[1,1024,256]{2,1,0:T(8,128)(2,1)}, u32[]{:S(2)}) copy-start(bf16[1,1024,256]{2,1,0:T(8,128)(2,1)} %param.5) | copy-start | bytes 1572868
  103.9 3.1 %copy-start.3 = (bf16[128,256]{1,0:T(8,128)(2,1)S(1)}, bf16[128,256]{1,0:T(8,128)(2,1)}, u32[]{:S(2)}) copy-start(bf16[128,256]{1,0:T(8,128)(2,1)} %param.7) | copy-start | bytes 196612
  107.0 95.4 %all-reduce.2.cloned.1.call-start = ((), (), s32[]{:S(2)}) async-start(), calls=%async_computation.2 | async-start | bytes 262144 | tf_op jit(solution)/shard_map/psum | solution.py:34
Sparse Core Ops, SparseCore 0:
  107.1 62.2 reduce-scatter.1
  171.7 30.6 all-reduce.1
where the time goes:
time: 211 us
  blocking collectives  123 us (58%)
  waiting for transfers between devices  55.3 us (26%)
  matrix products  14.4 us (7%)
  between operations  14.1 us (7%)
  other arithmetic  2.61 us (1%)
    all_gather x1, blocking collectives, per_device(): lax.all_gather(phi_param, 'seq', axis=0, tiled=True)  31.8 us
    all_gather x1, blocking collectives, per_device(): lax.all_gather(slot_grad[0], 'seq', axis=0, tiled=True)  31.5 us
    psum x1, waiting for transfers between devices, per_device(): phi_grad = lax.psum(phi_share, 'batch')  28.3 us
    reduce_scatter x1, waiting for transfers between devices, per_device(): lax.psum_scatter(phi_terms, 'seq', scatter_dimension=0, tiled=True)  26.9 us
    pmax x1, blocking collectives, per_device(): col_peak = lax.pmax(jnp.max(scores, axis=0, keepdims=True), 'seq')  23.2 us
    psum x1, blocking collectives, per_device(): lax.psum(jnp.sum(dispatch * weight_grad, axis=0, keepdims=True), 'seq')  19.4 us
    psum x1, blocking collectives, per_device(): col_total = lax.psum(jnp.sum(raw_weights, axis=0, keepdims=True), 'seq')  17.1 us
    dot_general x1, matrix products, per_device(): lax.dot_general(logit_grad, phi_full, (((1,), (1,)), ((), ())), preferred...  4.68 us
  transfers between devices with their start and end apart: 2, of which 2 were waited for; matrix products, arithmetic and copies ran while one was open for 4% of the time, Pallas kernels for 0%

commit v1 on v0

--- a/solution.py
+++ b/solution.py
@@ -1,10 +1,280 @@
+import functools
+
 import jax
 import jax.numpy as jnp
 from jax import lax
+from jax.experimental import pallas as pl
+from jax.experimental.pallas import tpu as pltpu
 from jax.sharding import PartitionSpec as P
 
-
-def per_device(tokens, logits, slot_grad, phi_param):
+MESH = pl.DeviceIdType.MESH
+F32 = jnp.float32
+BF16 = jnp.bfloat16
+
+
+def fused_kernel(
+    n, scale, tok_hbm, log_hbm, slot_hbm, phi_hbm, out_hbm, phi_out,
+    tok, log, raw, wg, gath, phig, stat, disp, lg, lgt, part, part_low, recv_a, sum_a, low_a,
+    recv_b, sum_b, low_b, recv_c, fin, tg,
+    load_sem, ag_send, ag_recv, fw_send, fw_recv, st_send, st_recv, ph_send, ph_recv,
+    pb_send, pb_recv, ab_send, ab_recv, c_send, c_recv, d_send, d_recv, out_sem,
+):
+    me = lax.axis_index("seq")
+    bat = lax.axis_index("batch")
+    half = n // 2
+    twin = me + 1 - 2 * (me % 2)
+    bat_a = bat + 1 - 2 * (bat % 2)
+    bat_b = (bat + 2) % 4
+    bat_c = (bat_a + 2) % 4
+    keep_a = bat % 2
+    keep_b = bat // 2
+    rows = tok.shape[0]
+    step = min(256, rows)
+    steps = rows // step
+
+    def remote(src, dst, send, recv, seq_at, bat_at):
+        return pltpu.make_async_remote_copy(
+            src_ref=src, dst_ref=dst, send_sem=send, recv_sem=recv,
+            device_id=(seq_at, bat_at), device_id_type=MESH,
+        )
+
+    load_slot = pltpu.make_async_copy(slot_hbm, gath.at[me], load_sem.at[0])
+    load_log = pltpu.make_async_copy(log_hbm, log, load_sem.at[1])
+    load_phi = pltpu.make_async_copy(phi_hbm.at[bat], phig.at[me, bat], load_sem.at[2])
+    load_tok = pltpu.make_async_copy(tok_hbm, tok, load_sem.at[3])
+    load_slot.start()
+    load_log.start()
+    load_tok.start()
+    load_phi.start()
+
+    barrier = pltpu.get_barrier_semaphore()
+    for k in range(1, n):
+        pl.semaphore_signal(barrier, inc=1, device_id=((me + k) % n, bat), device_id_type=MESH)
+    for other in (bat_a, bat_b, bat_c):
+        pl.semaphore_signal(barrier, inc=1, device_id=(me, other), device_id_type=MESH)
+    pl.semaphore_wait(barrier, n - 1 + 3)
+
+    load_slot.wait()
+    to_twin = remote(gath.at[me], gath.at[me], fw_send.at[0], fw_recv.at[0], twin, bat)
+    to_twin.start()
+    direct = []
+    for k in range(1, half):
+        direct.append(remote(gath.at[me], gath.at[me], ag_send.at[k], ag_recv.at[k], (me + 2 * k) % n, bat))
+        direct[-1].start()
+
+    load_log.wait()
+
+    def chunk(i):
+        return pl.ds(pl.multiple_of(i * step, step), step)
+
+    def peak_step(i, top):
+        return jnp.maximum(top, jnp.max(log[chunk(i), :].astype(F32), axis=0, keepdims=True))
+
+    slots = log.shape[1]
+    peak = lax.fori_loop(0, steps, peak_step, jnp.full((1, slots), -jnp.inf, F32))
+
+    def exp_step(i, acc):
+        values = jnp.exp(log[chunk(i), :].astype(F32) - peak)
+        raw[chunk(i), :] = values
+        return acc + jnp.sum(values, axis=0, keepdims=True)
+
+    total = lax.fori_loop(0, steps, exp_step, jnp.zeros((1, slots), F32))
+
+    load_tok.wait()
+    relayed = []
+    for k in range(1, half):
+        source = (me - 2 * k + n) % n
+        direct[k - 1].wait_recv()
+        relayed.append(remote(gath.at[source], gath.at[source], fw_send.at[k], fw_recv.at[k], twin, bat))
+        relayed[-1].start()
+    to_twin.wait_recv()
+    for move in relayed:
+        move.wait_recv()
+
+    upstream = gath.reshape(slots, gath.shape[2])
+
+    def wg_step(i, acc):
+        values = lax.dot_general(
+            tok[chunk(i), :], upstream[...], (((1,), (1,)), ((), ())), preferred_element_type=F32
+        )
+        wg[chunk(i), :] = values
+        return acc + jnp.sum(values * raw[chunk(i), :], axis=0, keepdims=True)
+
+    dot = lax.fori_loop(0, steps, wg_step, jnp.zeros((1, slots), F32))
+
+    stat[me, 0:1, :] = peak
+    stat[me, 1:2, :] = total
+    stat[me, 2:3, :] = dot
+    stat_moves = []
+    for k in range(1, n):
+        stat_moves.append(remote(stat.at[me], stat.at[me], st_send.at[k], st_recv.at[k], (me + k) % n, bat))
+        stat_moves[-1].start()
+
+    load_phi.wait()
+    phi_moves = []
+    for k in range(1, n):
+        phi_moves.append(remote(phig.at[me, bat], phig.at[me, bat], ph_send.at[k], ph_recv.at[k], (me + k) % n, bat))
+        phi_moves[-1].start()
+
+    for move in stat_moves:
+        move.wait_recv()
+    peaks = stat[:, 0, :]
+    col_peak = jnp.max(peaks, axis=0, keepdims=True)
+    shifts = jnp.exp(peaks - col_peak)
+    col_total = jnp.sum(stat[:, 1, :] * shifts, axis=0, keepdims=True)
+    col_dot = jnp.sum(stat[:, 2, :] * shifts, axis=0, keepdims=True) / col_total
+    factor = jnp.exp(peak - col_peak) / col_total
+
+    def grad_step(i, carry):
+        weights = raw[chunk(i), :] * factor
+        grads = weights * (wg[chunk(i), :] - col_dot)
+        disp[chunk(i), :] = weights.astype(BF16)
+        lg[chunk(i), :] = grads.astype(BF16)
+        lgt[:, chunk(i)] = grads.T.astype(BF16)
+        return carry
+
+    lax.fori_loop(0, steps, grad_step, 0)
+
+    own = tok.shape[1] // n
+    quarter = slots // 4
+
+    for j in range(n // 2):
+        terms = jnp.dot(lgt[...], tok[:, 2 * own * j : 2 * own * (j + 1)], preferred_element_type=F32)
+        for side in range(2):
+            for qa in range(2):
+                for qb in range(2):
+                    at = (2 * qa + qb) * quarter
+                    block = terms[at : at + quarter, side * own : (side + 1) * own]
+                    part[qa, qb, 2 * j + side] = block
+                    part_low[qa, qb, 2 * j + side] = block.astype(BF16)
+    move_a = remote(part_low.at[1 - keep_a], recv_a, ab_send.at[0], ab_recv.at[0], me, bat_a)
+    move_a.start()
+    for move in phi_moves:
+        move.wait_recv()
+    move_a.wait_recv()
+    for qb in range(2):
+        for j in range(n):
+            block = part[keep_a, qb, j] + recv_a[qb, j].astype(F32)
+            sum_a[qb, j] = block
+            low_a[qb, j] = block.astype(BF16)
+    move_b = remote(low_a.at[1 - keep_b], recv_b, ab_send.at[1], ab_recv.at[1], me, bat_b)
+    move_b.start()
+    phi_b = remote(phig.at[:, bat], phig.at[:, bat], pb_send.at[0], pb_recv.at[0], me, bat_b)
+    phi_b.start()
+    move_b.wait_recv()
+    for j in range(n):
+        block = sum_a[keep_b, j] + recv_b[j].astype(F32)
+        sum_b[j] = block
+        low_b[j] = block.astype(BF16)
+    share_moves = []
+    for k in range(1, n):
+        target = (me + k) % n
+        share_moves.append(remote(low_b.at[target], recv_c.at[me], c_send.at[k], c_recv.at[k], target, bat))
+        share_moves[-1].start()
+
+    phi_b.wait_recv()
+    phi_a = [
+        remote(phig.at[:, bat], phig.at[:, bat], pb_send.at[1], pb_recv.at[1], me, bat_a),
+        remote(phig.at[:, bat_b], phig.at[:, bat_b], pb_send.at[2], pb_recv.at[2], me, bat_a),
+    ]
+    for move in phi_a:
+        move.start()
+    for move in phi_a:
+        move.wait_recv()
+
+    phi_full = phig.reshape(phig.shape[0] * phig.shape[1] * phig.shape[2], phig.shape[3])
+
+    def out_copy(i):
+        return pltpu.make_async_copy(tg.at[chunk(i), :], out_hbm.at[chunk(i), :], out_sem.at[i])
+
+    def out_step(i, carry):
+        values = jnp.dot(disp[chunk(i), :], upstream[...], preferred_element_type=F32)
+        values = values + lax.dot_general(
+            lg[chunk(i), :], phi_full[...], (((1,), (1,)), ((), ())), preferred_element_type=F32
+        )
+        tg[chunk(i), :] = (scale * values).astype(BF16)
+        out_copy(i).start()
+        return carry
+
+    lax.fori_loop(0, steps, out_step, 0)
+
+    share = sum_b[me]
+    for k in range(1, n):
+        share_moves[k - 1].wait_recv()
+        share = share + recv_c[(me - k + n) % n].astype(F32)
+    mine = 2 * keep_a + keep_b
+    fin[mine] = share
+    last = []
+    for k, other in enumerate((bat_c, bat_b, bat_a)):
+        last.append(remote(fin.at[mine], fin.at[mine], d_send.at[k], d_recv.at[k], me, other))
+        last[-1].start()
+    for move in last:
+        move.wait_recv()
+    phi_out[...] = fin[...].reshape(slots, own).T
+
+    for i in range(steps):
+        out_copy(i).wait()
+    for move in [to_twin, move_a, move_b, phi_b] + direct + relayed + stat_moves + phi_moves + share_moves + phi_a + last:
+        move.wait_send()
+
+
+def fused(n, tokens, logits, slot_grad, phi_param):
+    rows, width = tokens.shape
+    slots = logits.shape[1]
+    own = width // n
+    quarter = slots // 4
+    scale = float(n * rows // 16)
+    dma = pltpu.SemaphoreType.DMA
+    steps = rows // min(256, rows)
+    hbm = pl.BlockSpec(memory_space=pl.ANY)
+    return pl.pallas_call(
+        functools.partial(fused_kernel, n, scale),
+        out_shape=(
+            jax.ShapeDtypeStruct((rows, width), BF16),
+            jax.ShapeDtypeStruct((own, slots), F32),
+        ),
+        in_specs=[hbm] * 4,
+        out_specs=(hbm, pl.BlockSpec(memory_space=pltpu.VMEM)),
+        scratch_shapes=[
+            pltpu.VMEM((rows, width), BF16),
+            pltpu.VMEM((rows, slots), BF16),
+            pltpu.VMEM((rows, slots), F32),
+            pltpu.VMEM((rows, slots), F32),
+            pltpu.VMEM((n, slots // n, width), BF16),
+            pltpu.VMEM((n, 4, own // 4, slots), BF16),
+            pltpu.VMEM((n, 8, slots), F32),
+            pltpu.VMEM((rows, slots), BF16),
+            pltpu.VMEM((rows, slots), BF16),
+            pltpu.VMEM((slots, rows), BF16),
+            pltpu.VMEM((2, 2, n, quarter, own), F32),
+            pltpu.VMEM((2, 2, n, quarter, own), BF16),
+            pltpu.VMEM((2, n, quarter, own), BF16),
+            pltpu.VMEM((2, n, quarter, own), F32),
+            pltpu.VMEM((2, n, quarter, own), BF16),
+            pltpu.VMEM((n, quarter, own), BF16),
+            pltpu.VMEM((n, quarter, own), F32),
+            pltpu.VMEM((n, quarter, own), BF16),
+            pltpu.VMEM((n, quarter, own), BF16),
+            pltpu.VMEM((4, quarter, own), F32),
+            pltpu.VMEM((rows, width), BF16),
+            dma((4,)),
+            dma((n,)), dma((n,)),
+            dma((n,)), dma((n,)),
+            dma((n,)), dma((n,)),
+            dma((n,)), dma((n,)),
+            dma((3,)), dma((3,)),
+            dma((2,)), dma((2,)),
+            dma((n,)), dma((n,)),
+            dma((3,)), dma((3,)),
+            dma((steps,)),
+        ],
+        compiler_params=pltpu.CompilerParams(
+            collective_id=0, has_side_effects=True, vmem_limit_bytes=60 * 1024 * 1024
+        ),
+    )(tokens, logits, slot_grad, phi_param.reshape(4, own // 4, slots))
+
+
+def plain(tokens, logits, slot_grad, phi_param):
     inputs = tokens[0]
     scores = logits[0].astype(jnp.float32)
     upstream, phi_full = (
@@ -35,9 +305,17 @@
     return (token_grad, phi_grad)
 
 
+def per_device(n, batches, tokens, logits, slot_grad, phi_param):
+    own, slots = phi_param.shape
+    if batches == 4 and n % 2 == 0 and slot_grad.shape[1] % 16 == 0 and own % 128 == 0 and slots % 128 == 0 and tokens.shape[1] % 256 == 0:
+        token_grad, phi_grad = fused(n, tokens[0], logits[0], slot_grad[0], phi_param)
+        return token_grad[None], phi_grad
+    return plain(tokens, logits, slot_grad, phi_param)
+
+
 def solution(mesh):
     return jax.shard_map(
-        per_device,
+        functools.partial(per_device, mesh.shape["seq"], mesh.shape["batch"]),
         mesh=mesh,
         in_specs=(
             P("batch", "seq", None),

time: 211 us -> 44.5 us (0.21)
  blocking collectives: 123 us -> 0 us
  waiting for transfers between devices: 55.3 us -> 0 us
  Pallas kernels: 0 us -> 40 us
  matrix products: 14.4 us -> 0 us
  between operations: 14.1 us -> 0.65 us
  other arithmetic: 2.61 us -> 0 us
    all_gather x2 -> x0, blocking collectives: 63.2 us -> none  [the longest x1 31.8 us: per_device(): lax.all_gather(phi_param, 'seq', axis=0, tiled=True)]
    pallas_call x0 -> x1, Pallas kernels: none -> 40 us  [fused(): pl.pallas_call(functools.partial(fused_kernel, n, scale), out_shape=(jax....]
    psum x2 -> x0, blocking collectives: 36.5 us -> none  [the longest x1 19.4 us: per_device(): lax.psum(jnp.sum(dispatch * weight_grad, axis=0, keepdims=True), 'seq')]
    psum x1 -> x0, waiting for transfers between devices: 28.3 us -> none  [per_device(): phi_grad = lax.psum(phi_share, 'batch')]
    reduce_scatter x1 -> x0, waiting for transfers between devices: 26.9 us -> none  [per_device(): lax.psum_scatter(phi_terms, 'seq', scatter_dimension=0, tiled=True)]
    pmax x1 -> x0, blocking collectives: 23.2 us -> none  [per_device(): col_peak = lax.pmax(jnp.max(scores, axis=0, keepdims=True), 'seq')]
    dot_general x4 -> x0, matrix products: 14.4 us -> none  [the longest x1 4.68 us: per_device(): lax.dot_general(logit_grad, phi_full, (((1,), (1,)), ((), ())), preferred...]
  transfers between devices with their start and end apart: 2 -> 0, of which waited for: 2 -> 0; matrix products, arithmetic and copies ran while one was open for 4% -> 0% of each run, Pallas kernels for 0% -> 0%
where the time goes in v1:
time: 44.5 us; the launch traced here: 44.4 us
  Pallas kernels  40 us (90%)
  local copies, waits for them, and re-layouts  3.77 us (8%)
  between operations  0.65 us (1%)
    pallas_call x1, Pallas kernels, fused(): pl.pallas_call(functools.partial(fused_kernel, n, scale), out_shape=(jax....  40 us
    unnamed x4, local copies, waits for them, and re-layouts  3.77 us

profile of v1, /device:TPU:0, one launch (start us, length us, event | category | flops | bytes accessed | tf_op | source)
XLA Modules:
  0.0 44.4 jit_solution(9455461098145502966)
XLA Ops:
  0.6 40.0 %shard_map.59 = (bf16[1024,1024]{1,0:T(8,128)(2,1)}, f32[128,256]{1,0:T(8,128)}) custom-call(bf16[1024,1024]{1,0:T(8,128)(2,1)} %bitcast.5, bf16[1024,256]{1,0:T(8,128)(2,1)} %bitcast.7, bf16[32,1024]{1,0:T(8,128)(2,1)} %bitcast.8, bf16[4,32,256]{2,1,0:T(8,128)(2,1)} %bitcast.9), custom_call_target="tpu_custom_call" | custom-call | tf_op jit(solution)/shard_map/pallas_call | solution.py:230
  40.6 0.0 copy-start
  40.6 3.1 %copy.8 = bf16[1,1024,1024]{2,1,0:T(8,128)(2,1)} copy(bf16[1,1024,1024]{2,1,0:T(8,128)(2,1)} %bitcast.6) | data formatting | bytes 4194304
  43.7 0.0 copy-done
  43.7 0.7 %copy.9 = f32[128,256]{1,0:T(8,128)} copy(f32[128,256]{1,0:T(8,128)S(1)} %copy-done) | data formatting | bytes 262144
Async XLA Ops:
  40.6 3.1 %copy-start = (f32[128,256]{1,0:T(8,128)S(1)}, f32[128,256]{1,0:T(8,128)}, u32[]{:S(2)}) copy-start(f32[128,256]{1,0:T(8,128)} %get-tuple-element.9) | copy-start | bytes 393220

commit v2 on v1

--- a/solution.py
+++ b/solution.py
@@ -13,11 +13,11 @@
 
 
 def fused_kernel(
-    n, scale, tok_hbm, log_hbm, slot_hbm, phi_hbm, out_hbm, phi_out,
+    n, scale, tok_hbm, log_hbm, slot_hbm, phi_hbm, tok_out, phi_out,
     tok, log, raw, wg, gath, phig, stat, disp, lg, lgt, part, part_low, recv_a, sum_a, low_a,
-    recv_b, sum_b, low_b, recv_c, fin, tg,
+    recv_b, sum_b, low_b, recv_c, fin,
     load_sem, ag_send, ag_recv, fw_send, fw_recv, st_send, st_recv, ph_send, ph_recv,
-    pb_send, pb_recv, ab_send, ab_recv, c_send, c_recv, d_send, d_recv, out_sem,
+    pb_send, pb_recv, a_send, a_recv, b_send, b_recv, c_send, c_recv, d_send, d_recv,
 ):
     me = lax.axis_index("seq")
     bat = lax.axis_index("batch")
@@ -55,12 +55,20 @@
     pl.semaphore_wait(barrier, n - 1 + 3)
 
     load_slot.wait()
-    to_twin = remote(gath.at[me], gath.at[me], fw_send.at[0], fw_recv.at[0], twin, bat)
-    to_twin.start()
+    pieces = 2 if gath.shape[1] % 32 == 0 else 1
+    piece = gath.shape[1] // pieces
+
+    def shard(j, h):
+        return gath.at[j, pl.ds(h * piece, piece)]
+
+    to_twin = []
     direct = []
-    for k in range(1, half):
-        direct.append(remote(gath.at[me], gath.at[me], ag_send.at[k], ag_recv.at[k], (me + 2 * k) % n, bat))
-        direct[-1].start()
+    for h in range(pieces):
+        to_twin.append(remote(shard(me, h), shard(me, h), fw_send.at[0, h], fw_recv.at[0, h], twin, bat))
+        to_twin[-1].start()
+        for k in range(1, half):
+            direct.append(remote(shard(me, h), shard(me, h), ag_send.at[k, h], ag_recv.at[k, h], (me + 2 * k) % n, bat))
+            direct[-1].start()
 
     load_log.wait()
 
@@ -82,13 +90,13 @@
 
     load_tok.wait()
     relayed = []
-    for k in range(1, half):
-        source = (me - 2 * k + n) % n
-        direct[k - 1].wait_recv()
-        relayed.append(remote(gath.at[source], gath.at[source], fw_send.at[k], fw_recv.at[k], twin, bat))
-        relayed[-1].start()
-    to_twin.wait_recv()
-    for move in relayed:
+    for h in range(pieces):
+        for k in range(1, half):
+            source = (me - 2 * k + n) % n
+            direct[h * (half - 1) + k - 1].wait_recv()
+            relayed.append(remote(shard(source, h), shard(source, h), fw_send.at[k, h], fw_recv.at[k, h], twin, bat))
+            relayed[-1].start()
+    for move in to_twin + relayed:
         move.wait_recv()
 
     upstream = gath.reshape(slots, gath.shape[2])
@@ -138,39 +146,51 @@
     own = tok.shape[1] // n
     quarter = slots // 4
 
-    for j in range(n // 2):
-        terms = jnp.dot(lgt[...], tok[:, 2 * own * j : 2 * own * (j + 1)], preferred_element_type=F32)
-        for side in range(2):
-            for qa in range(2):
-                for qb in range(2):
-                    at = (2 * qa + qb) * quarter
-                    block = terms[at : at + quarter, side * own : (side + 1) * own]
-                    part[qa, qb, 2 * j + side] = block
-                    part_low[qa, qb, 2 * j + side] = block.astype(BF16)
-    move_a = remote(part_low.at[1 - keep_a], recv_a, ab_send.at[0], ab_recv.at[0], me, bat_a)
-    move_a.start()
+    group = n // 2
+    owners = [[j for j in range(n) if (n // 4 <= j < n - n // 4) == bool(g)] for g in range(2)]
+    moves_a = []
+    for g in range(2):
+        for at in range(0, group, 2):
+            j = owners[g][at]
+            terms = jnp.dot(lgt[...], tok[:, own * j : own * (j + 2)], preferred_element_type=F32)
+            for side in range(2):
+                for qa in range(2):
+                    for qb in range(2):
+                        first = (2 * qa + qb) * quarter
+                        block = terms[first : first + quarter, side * own : (side + 1) * own]
+                        part[g, qa, qb, at + side] = block
+                        part_low[g, qa, qb, at + side] = block.astype(BF16)
+        moves_a.append(remote(part_low.at[g, 1 - keep_a], recv_a.at[g], a_send.at[g], a_recv.at[g], me, bat_a))
+        moves_a[-1].start()
+    moves_b = []
+    for g in range(2):
+        moves_a[g].wait_recv()
+        for qb in range(2):
+            for at in range(group):
+                block = part[g, keep_a, qb, at] + recv_a[g, qb, at].astype(F32)
+                sum_a[g, qb, at] = block
+                low_a[g, qb, at] = block.astype(BF16)
+        moves_b.append(remote(low_a.at[g, 1 - keep_b], recv_b.at[g], b_send.at[g], b_recv.at[g], me, bat_b))
+        moves_b[-1].start()
     for move in phi_moves:
         move.wait_recv()
-    move_a.wait_recv()
-    for qb in range(2):
-        for j in range(n):
-            block = part[keep_a, qb, j] + recv_a[qb, j].astype(F32)
-            sum_a[qb, j] = block
-            low_a[qb, j] = block.astype(BF16)
-    move_b = remote(low_a.at[1 - keep_b], recv_b, ab_send.at[1], ab_recv.at[1], me, bat_b)
-    move_b.start()
     phi_b = remote(phig.at[:, bat], phig.at[:, bat], pb_send.at[0], pb_recv.at[0], me, bat_b)
     phi_b.start()
-    move_b.wait_recv()
-    for j in range(n):
-        block = sum_a[keep_b, j] + recv_b[j].astype(F32)
-        sum_b[j] = block
-        low_b[j] = block.astype(BF16)
-    share_moves = []
-    for k in range(1, n):
-        target = (me + k) % n
-        share_moves.append(remote(low_b.at[target], recv_c.at[me], c_send.at[k], c_recv.at[k], target, bat))
-        share_moves[-1].start()
+
+    def share_move(g, at):
+        j = owners[g][at]
+        return remote(low_b.at[g, at], recv_c.at[me], c_send.at[j], c_recv.at[me], j, bat)
+
+    for g in range(2):
+        moves_b[g].wait_recv()
+        for at in range(group):
+            block = sum_a[g, keep_b, at] + recv_b[g, at].astype(F32)
+            sum_b[owners[g][at]] = block
+            low_b[g, at] = block.astype(BF16)
+        for at in range(group):
+            @pl.when(me != owners[g][at])
+            def _(g=g, at=at):
+                share_move(g, at).start()
 
     phi_b.wait_recv()
     phi_a = [
@@ -179,42 +199,42 @@
     ]
     for move in phi_a:
         move.start()
-    for move in phi_a:
-        move.wait_recv()
-
-    phi_full = phig.reshape(phig.shape[0] * phig.shape[1] * phig.shape[2], phig.shape[3])
-
-    def out_copy(i):
-        return pltpu.make_async_copy(tg.at[chunk(i), :], out_hbm.at[chunk(i), :], out_sem.at[i])
-
-    def out_step(i, carry):
-        values = jnp.dot(disp[chunk(i), :], upstream[...], preferred_element_type=F32)
-        values = values + lax.dot_general(
-            lg[chunk(i), :], phi_full[...], (((1,), (1,)), ((), ())), preferred_element_type=F32
-        )
-        tg[chunk(i), :] = (scale * values).astype(BF16)
-        out_copy(i).start()
-        return carry
-
-    lax.fori_loop(0, steps, out_step, 0)
-
     share = sum_b[me]
     for k in range(1, n):
-        share_moves[k - 1].wait_recv()
-        share = share + recv_c[(me - k + n) % n].astype(F32)
+        source = (me - k + n) % n
+        remote(low_b.at[0, 0], recv_c.at[source], c_send.at[0], c_recv.at[source], source, bat).wait_recv()
+        share = share + recv_c[source].astype(F32)
     mine = 2 * keep_a + keep_b
     fin[mine] = share
     last = []
     for k, other in enumerate((bat_c, bat_b, bat_a)):
         last.append(remote(fin.at[mine], fin.at[mine], d_send.at[k], d_recv.at[k], me, other))
         last[-1].start()
+    for move in phi_a:
+        move.wait_recv()
+
+    phi_full = phig.reshape(phig.shape[0] * phig.shape[1] * phig.shape[2], phig.shape[3])
+
+    def out_step(i, carry):
+        values = jnp.dot(disp[chunk(i), :], upstream[...], preferred_element_type=F32)
+        values = values + lax.dot_general(
+            lg[chunk(i), :], phi_full[...], (((1,), (1,)), ((), ())), preferred_element_type=F32
+        )
+        tok_out[chunk(i), :] = (scale * values).astype(BF16)
+        return carry
+
+    lax.fori_loop(0, steps, out_step, 0)
+
     for move in last:
         move.wait_recv()
     phi_out[...] = fin[...].reshape(slots, own).T
 
-    for i in range(steps):
-        out_copy(i).wait()
-    for move in [to_twin, move_a, move_b, phi_b] + direct + relayed + stat_moves + phi_moves + share_moves + phi_a + last:
+    for g in range(2):
+        for at in range(group):
+            @pl.when(me != owners[g][at])
+            def _(g=g, at=at):
+                share_move(g, at).wait_send()
+    for move in to_twin + direct + relayed + stat_moves + phi_moves + moves_a + moves_b + [phi_b] + phi_a + last:
         move.wait_send()
 
 
@@ -225,8 +245,7 @@
     quarter = slots // 4
     scale = float(n * rows // 16)
     dma = pltpu.SemaphoreType.DMA
-    steps = rows // min(256, rows)
-    hbm = pl.BlockSpec(memory_space=pl.ANY)
+    hbm = pl.BlockSpec(memory_space=pltpu.HBM)
     return pl.pallas_call(
         functools.partial(fused_kernel, n, scale),
         out_shape=(
@@ -234,7 +253,7 @@
             jax.ShapeDtypeStruct((own, slots), F32),
         ),
         in_specs=[hbm] * 4,
-        out_specs=(hbm, pl.BlockSpec(memory_space=pltpu.VMEM)),
+        out_specs=(pl.BlockSpec(memory_space=pltpu.VMEM), pl.BlockSpec(memory_space=pltpu.VMEM)),
         scratch_shapes=[
             pltpu.VMEM((rows, width), BF16),
             pltpu.VMEM((rows, slots), BF16),
@@ -246,30 +265,29 @@
             pltpu.VMEM((rows, slots), BF16),
             pltpu.VMEM((rows, slots), BF16),
             pltpu.VMEM((slots, rows), BF16),
-            pltpu.VMEM((2, 2, n, quarter, own), F32),
-            pltpu.VMEM((2, 2, n, quarter, own), BF16),
-            pltpu.VMEM((2, n, quarter, own), BF16),
-            pltpu.VMEM((2, n, quarter, own), F32),
-            pltpu.VMEM((2, n, quarter, own), BF16),
-            pltpu.VMEM((n, quarter, own), BF16),
+            pltpu.VMEM((2, 2, 2, n // 2, quarter, own), F32),
+            pltpu.VMEM((2, 2, 2, n // 2, quarter, own), BF16),
+            pltpu.VMEM((2, 2, n // 2, quarter, own), BF16),
+            pltpu.VMEM((2, 2, n // 2, quarter, own), F32),
+            pltpu.VMEM((2, 2, n // 2, quarter, own), BF16),
+            pltpu.VMEM((2, n // 2, quarter, own), BF16),
             pltpu.VMEM((n, quarter, own), F32),
-            pltpu.VMEM((n, quarter, own), BF16),
+            pltpu.VMEM((2, n // 2, quarter, own), BF16),
             pltpu.VMEM((n, quarter, own), BF16),
             pltpu.VMEM((4, quarter, own), F32),
-            pltpu.VMEM((rows, width), BF16),
             dma((4,)),
-            dma((n,)), dma((n,)),
-            dma((n,)), dma((n,)),
+            dma((n // 2, 2)), dma((n // 2, 2)),
+            dma((n // 2, 2)), dma((n // 2, 2)),
             dma((n,)), dma((n,)),
             dma((n,)), dma((n,)),
             dma((3,)), dma((3,)),
             dma((2,)), dma((2,)),
+            dma((2,)), dma((2,)),
             dma((n,)), dma((n,)),
             dma((3,)), dma((3,)),
-            dma((steps,)),
         ],
         compiler_params=pltpu.CompilerParams(
-            collective_id=0, has_side_effects=True, vmem_limit_bytes=60 * 1024 * 1024
+            collective_id=0, has_side_effects=True, vmem_limit_bytes=52_000_000
         ),
     )(tokens, logits, slot_grad, phi_param.reshape(4, own // 4, slots))
 
@@ -307,7 +325,7 @@
 
 def per_device(n, batches, tokens, logits, slot_grad, phi_param):
     own, slots = phi_param.shape
-    if batches == 4 and n % 2 == 0 and slot_grad.shape[1] % 16 == 0 and own % 128 == 0 and slots % 128 == 0 and tokens.shape[1] % 256 == 0:
+    if batches == 4 and n % 8 == 0 and slot_grad.shape[1] % 16 == 0 and own % 128 == 0 and slots % 128 == 0 and tokens.shape[1] % 256 == 0:
         token_grad, phi_grad = fused(n, tokens[0], logits[0], slot_grad[0], phi_param)
         return token_grad[None], phi_grad
     return plain(tokens, logits, slot_grad, phi_param)

time: 44.5 us -> 41.5 us (0.933)
  Pallas kernels: 40 us -> 35.9 us
  local copies, waits for them, and re-layouts: 3.77 us -> 4.69 us
    pallas_call x1, Pallas kernels: 40 us -> 35.9 us  [fused(): pl.pallas_call(functools.partial(fused_kernel, n, scale), out_shape=(jax....]
    unnamed x4 -> x8, local copies, waits for them, and re-layouts: 3.77 us -> 4.69 us
where the time goes in v2:
time: 41.5 us; the launch traced here: 41.3 us
  Pallas kernels  35.9 us (87%)
  local copies, waits for them, and re-layouts  4.69 us (11%)
  between operations  0.65 us (2%)
    pallas_call x1, Pallas kernels, fused(): pl.pallas_call(functools.partial(fused_kernel, n, scale), out_shape=(jax....  35.9 us
    unnamed x8, local copies, waits for them, and re-layouts  4.69 us

profile of v2, /device:TPU:0, one launch (start us, length us, event | category | flops | bytes accessed | tf_op | source)
XLA Modules:
  0.0 41.3 jit_solution(3826893572503852986)
XLA Ops:
  0.6 0.0 copy-start
  0.6 1.0 %copy-done = bf16[1,1024,256]{2,1,0:T(8,128)(2,1)S(1)} copy-done((bf16[1,1024,256]{2,1,0:T(8,128)(2,1)S(1)}, bf16[1,1024,256]{2,1,0:T(8,128)(2,1)}, u32[]{:S(2)}) %copy-start) | copy-done | bytes 524312
  1.7 0.0 copy-start.1
  1.7 0.8 %copy-done.1 = bf16[1,32,1024]{2,1,0:T(8,128)(2,1)S(1)} copy-done((bf16[1,32,1024]{2,1,0:T(8,128)(2,1)S(1)}, bf16[1,32,1024]{2,1,0:T(8,128)(2,1)}, u32[]{:S(2)}) %copy-start.1) | copy-done | bytes 65560
  2.5 0.0 copy-start.2
  2.5 0.8 %copy-done.2 = bf16[128,256]{1,0:T(8,128)(2,1)S(1)} copy-done((bf16[128,256]{1,0:T(8,128)(2,1)S(1)}, bf16[128,256]{1,0:T(8,128)(2,1)}, u32[]{:S(2)}) %copy-start.2) | copy-done | bytes 65560
  3.4 35.9 %shard_map.59 = (bf16[1024,1024]{1,0:T(8,128)(2,1)S(1)}, f32[128,256]{1,0:T(8,128)S(1)}) custom-call(bf16[1024,1024]{1,0:T(8,128)(2,1)} %bitcast.9, bf16[1024,256]{1,0:T(8,128)(2,1)S(1)} %bitcast.6, bf16[32,1024]{1,0:T(8,128)(2,1)S(1)} %bitcast.7, bf16[4,32,256]{2,1,0:T(8,128)(2,1)S(1)} %bitcast.8), custom_call_target="tpu_custom_call" | custom-call | tf_op jit(solution)/shard_map/pallas_call | solution.py:249
  39.3 1.3 %copy.8 = bf16[1,1024,1024]{2,1,0:T(8,128)(2,1)} copy(bf16[1,1024,1024]{2,1,0:T(8,128)(2,1)S(1)} %bitcast.5) | data formatting | bytes 4194304
  40.6 0.7 %copy.9 = f32[128,256]{1,0:T(8,128)} copy(f32[128,256]{1,0:T(8,128)S(1)} %get-tuple-element.9) | data formatting | bytes 262144
Async XLA Ops:
  0.6 1.0 %copy-start = (bf16[1,1024,256]{2,1,0:T(8,128)(2,1)S(1)}, bf16[1,1024,256]{2,1,0:T(8,128)(2,1)}, u32[]{:S(2)}) copy-start(bf16[1,1024,256]{2,1,0:T(8,128)(2,1)} %param.5) | copy-start | bytes 1572868
  1.7 0.8 %copy-start.1 = (bf16[1,32,1024]{2,1,0:T(8,128)(2,1)S(1)}, bf16[1,32,1024]{2,1,0:T(8,128)(2,1)}, u32[]{:S(2)}) copy-start(bf16[1,32,1024]{2,1,0:T(8,128)(2,1)} %param.6) | copy-start | bytes 196612
  2.5 0.8 %copy-start.2 = (bf16[128,256]{1,0:T(8,128)(2,1)S(1)}, bf16[128,256]{1,0:T(8,128)(2,1)}, u32[]{:S(2)}) copy-start(bf16[128,256]{1,0:T(8,128)(2,1)} %param.7) | copy-start | bytes 196612

commit v3 on v2

--- a/solution.py
+++ b/solution.py
@@ -289,7 +289,10 @@
         compiler_params=pltpu.CompilerParams(
             collective_id=0, has_side_effects=True, vmem_limit_bytes=52_000_000
         ),
-    )(tokens, logits, slot_grad, phi_param.reshape(4, own // 4, slots))
+    )(*[
+        pltpu.with_memory_space_constraint(x, pltpu.HBM)
+        for x in (tokens, logits, slot_grad, phi_param.reshape(4, own // 4, slots))
+    ])
 
 
 def plain(tokens, logits, slot_grad, phi_param):

time: 41.5 us -> 38.6 us (0.930)
  local copies, waits for them, and re-layouts: 4.69 us -> 1.98 us
    unnamed x8 -> x2, local copies, waits for them, and re-layouts: 4.69 us -> 1.98 us
where the time goes in v3:
time: 38.6 us; the launch traced here: 38.5 us
  Pallas kernels  35.8 us (93%)
  local copies, waits for them, and re-layouts  1.98 us (5%)
  between operations  0.64 us (2%)
    pallas_call x1, Pallas kernels, fused(): pl.pallas_call(functools.partial(fused_kernel, n, scale), out_shape=(jax....  35.8 us
    unnamed x2, local copies, waits for them, and re-layouts  1.98 us

profile of v3, /device:TPU:0, one launch (start us, length us, event | category | flops | bytes accessed | tf_op | source)
XLA Modules:
  0.0 38.5 jit_solution(4634347229094089438)
XLA Ops:
  0.6 35.8 %shard_map.59 = (bf16[1024,1024]{1,0:T(8,128)(2,1)S(1)}, f32[128,256]{1,0:T(8,128)S(1)}) custom-call(bf16[1024,1024]{1,0:T(8,128)(2,1)} %bitcast.6, bf16[1024,256]{1,0:T(8,128)(2,1)} %bitcast.7, bf16[32,1024]{1,0:T(8,128)(2,1)} %bitcast.8, bf16[4,32,256]{2,1,0:T(8,128)(2,1)} %bitcast.9), custom_call_target="tpu_custom_call" | custom-call | tf_op jit(solution)/shard_map/pallas_call | solution.py:249
  36.5 1.3 %copy.8 = bf16[1,1024,1024]{2,1,0:T(8,128)(2,1)} copy(bf16[1,1024,1024]{2,1,0:T(8,128)(2,1)S(1)} %bitcast.5) | data formatting | bytes 4194304
  37.8 0.7 %copy.9 = f32[128,256]{1,0:T(8,128)} copy(f32[128,256]{1,0:T(8,128)S(1)} %get-tuple-element.9) | data formatting | bytes 262144

commit v4 on v3

--- a/solution.py
+++ b/solution.py
@@ -61,13 +61,22 @@
     def shard(j, h):
         return gath.at[j, pl.ds(h * piece, piece)]
 
+    place = me // 2
+    low = 1 - place // (half // 2)
+
+    def column_peer(i):
+        at = low * (half - 1 - i) + (1 - low) * i
+        return at - low * ((place - at + half) // half) + (1 - low) * ((at - place + half) // half)
+
     to_twin = []
     direct = []
     for h in range(pieces):
-        to_twin.append(remote(shard(me, h), shard(me, h), fw_send.at[0, h], fw_recv.at[0, h], twin, bat))
+        to_twin.append(remote(shard(me, h), shard(me, h), fw_send.at[0, h], fw_recv.at[me // 2, h], twin, bat))
         to_twin[-1].start()
         for k in range(1, half):
-            direct.append(remote(shard(me, h), shard(me, h), ag_send.at[k, h], ag_recv.at[k, h], (me + 2 * k) % n, bat))
+            target = column_peer(k - 1)
+            direct.append(remote(
+                shard(me, h), shard(me, h), ag_send.at[k, h], ag_recv.at[me // 2, h], 2 * target + me % 2, bat))
             direct[-1].start()
 
     load_log.wait()
@@ -92,23 +101,32 @@
     relayed = []
     for h in range(pieces):
         for k in range(1, half):
-            source = (me - 2 * k + n) % n
-            direct[h * (half - 1) + k - 1].wait_recv()
-            relayed.append(remote(shard(source, h), shard(source, h), fw_send.at[k, h], fw_recv.at[k, h], twin, bat))
+            origin = column_peer(k - 1)
+            source = 2 * origin + me % 2
+            remote(shard(source, h), shard(source, h), ag_send.at[k, h], ag_recv.at[origin, h], source, bat).wait_recv()
+            relayed.append(
+                remote(shard(source, h), shard(source, h), fw_send.at[k, h], fw_recv.at[origin, h], twin, bat))
             relayed[-1].start()
-    for move in to_twin + relayed:
-        move.wait_recv()
+    for h in range(pieces):
+        for j in range(half):
+            source = 2 * j + twin % 2
+            remote(shard(source, h), shard(source, h), fw_send.at[0, h], fw_recv.at[j, h], twin, bat).wait_recv()
 
     upstream = gath.reshape(slots, gath.shape[2])
+
+    large = 2 * step if rows % (2 * step) == 0 else step
+
+    def wide(i):
+        return pl.ds(pl.multiple_of(i * large, large), large)
 
     def wg_step(i, acc):
         values = lax.dot_general(
-            tok[chunk(i), :], upstream[...], (((1,), (1,)), ((), ())), preferred_element_type=F32
+            tok[wide(i), :], upstream[...], (((1,), (1,)), ((), ())), preferred_element_type=F32
         )
-        wg[chunk(i), :] = values
-        return acc + jnp.sum(values * raw[chunk(i), :], axis=0, keepdims=True)
-
-    dot = lax.fori_loop(0, steps, wg_step, jnp.zeros((1, slots), F32))
+        wg[wide(i), :] = values
+        return acc + jnp.sum(values * raw[wide(i), :], axis=0, keepdims=True)
+
+    dot = lax.fori_loop(0, rows // large, wg_step, jnp.zeros((1, slots), F32))
 
     stat[me, 0:1, :] = peak
     stat[me, 1:2, :] = total
@@ -216,14 +234,14 @@
     phi_full = phig.reshape(phig.shape[0] * phig.shape[1] * phig.shape[2], phig.shape[3])
 
     def out_step(i, carry):
-        values = jnp.dot(disp[chunk(i), :], upstream[...], preferred_element_type=F32)
+        values = jnp.dot(disp[wide(i), :], upstream[...], preferred_element_type=F32)
         values = values + lax.dot_general(
-            lg[chunk(i), :], phi_full[...], (((1,), (1,)), ((), ())), preferred_element_type=F32
+            lg[wide(i), :], phi_full[...], (((1,), (1,)), ((), ())), preferred_element_type=F32
         )
-        tok_out[chunk(i), :] = (scale * values).astype(BF16)
+        tok_out[wide(i), :] = (scale * values).astype(BF16)
         return carry
 
-    lax.fori_loop(0, steps, out_step, 0)
+    lax.fori_loop(0, rows // large, out_step, 0)
 
     for move in last:
         move.wait_recv()

time: 38.6 us -> 37.9 us (0.982)
  Pallas kernels: 35.8 us -> 35.2 us
    pallas_call x1, Pallas kernels: 35.8 us -> 35.2 us  [fused(): pl.pallas_call(functools.partial(fused_kernel, n, scale), out_shape=(jax....]
where the time goes in v4:
time: 37.9 us; the launch traced here: 37.8 us
  Pallas kernels  35.2 us (93%)
  local copies, waits for them, and re-layouts  1.98 us (5%)
  between operations  0.64 us (2%)
    pallas_call x1, Pallas kernels, fused(): pl.pallas_call(functools.partial(fused_kernel, n, scale), out_shape=(jax....  35.2 us
    unnamed x2, local copies, waits for them, and re-layouts  1.98 us

profile of v4, /device:TPU:0, one launch (start us, length us, event | category | flops | bytes accessed | tf_op | source)
XLA Modules:
  0.0 37.8 jit_solution(1828931443452188845)
XLA Ops:
  0.6 35.2 %shard_map.59 = (bf16[1024,1024]{1,0:T(8,128)(2,1)S(1)}, f32[128,256]{1,0:T(8,128)S(1)}) custom-call(bf16[1024,1024]{1,0:T(8,128)(2,1)} %bitcast.6, bf16[1024,256]{1,0:T(8,128)(2,1)} %bitcast.7, bf16[32,1024]{1,0:T(8,128)(2,1)} %bitcast.8, bf16[4,32,256]{2,1,0:T(8,128)(2,1)} %bitcast.9), custom_call_target="tpu_custom_call" | custom-call | tf_op jit(solution)/shard_map/pallas_call | solution.py:267
  35.8 1.3 %copy.8 = bf16[1,1024,1024]{2,1,0:T(8,128)(2,1)} copy(bf16[1,1024,1024]{2,1,0:T(8,128)(2,1)S(1)} %bitcast.5) | data formatting | bytes 4194304
  37.1 0.7 %copy.9 = f32[128,256]{1,0:T(8,128)} copy(f32[128,256]{1,0:T(8,128)S(1)} %get-tuple-element.9) | data formatting | bytes 262144

commit v5 on v4

--- a/solution.py
+++ b/solution.py
@@ -14,7 +14,7 @@
 
 def fused_kernel(
     n, scale, tok_hbm, log_hbm, slot_hbm, phi_hbm, tok_out, phi_out,
-    tok, log, raw, wg, gath, phig, stat, disp, lg, lgt, part, part_low, recv_a, sum_a, low_a,
+    tok, log, raw, wg, gath, phig, stat, disp, lg, tokt, part, part_low, recv_a, sum_a, low_a,
     recv_b, sum_b, low_b, recv_c, fin,
     load_sem, ag_send, ag_recv, fw_send, fw_recv, st_send, st_recv, ph_send, ph_recv,
     pb_send, pb_recv, a_send, a_recv, b_send, b_recv, c_send, c_recv, d_send, d_recv,
@@ -98,6 +98,12 @@
     total = lax.fori_loop(0, steps, exp_step, jnp.zeros((1, slots), F32))
 
     load_tok.wait()
+
+    def turn_step(i, carry):
+        tokt[:, chunk(i)] = tok[chunk(i), :].T
+        return carry
+
+    lax.fori_loop(0, steps, turn_step, 0)
     relayed = []
     for h in range(pieces):
         for k in range(1, half):
@@ -156,13 +162,12 @@
         grads = weights * (wg[chunk(i), :] - col_dot)
         disp[chunk(i), :] = weights.astype(BF16)
         lg[chunk(i), :] = grads.astype(BF16)
-        lgt[:, chunk(i)] = grads.T.astype(BF16)
         return carry
 
     lax.fori_loop(0, steps, grad_step, 0)
 
     own = tok.shape[1] // n
-    quarter = slots // 4
+    quarter = own // 4
 
     group = n // 2
     owners = [[j for j in range(n) if (n // 4 <= j < n - n // 4) == bool(g)] for g in range(2)]
@@ -170,12 +175,12 @@
     for g in range(2):
         for at in range(0, group, 2):
             j = owners[g][at]
-            terms = jnp.dot(lgt[...], tok[:, own * j : own * (j + 2)], preferred_element_type=F32)
+            terms = jnp.dot(tokt[own * j : own * (j + 2), :], lg[...], preferred_element_type=F32)
             for side in range(2):
                 for qa in range(2):
                     for qb in range(2):
-                        first = (2 * qa + qb) * quarter
-                        block = terms[first : first + quarter, side * own : (side + 1) * own]
+                        first = own * side + (2 * qa + qb) * quarter
+                        block = terms[first : first + quarter, :]
                         part[g, qa, qb, at + side] = block
                         part_low[g, qa, qb, at + side] = block.astype(BF16)
         moves_a.append(remote(part_low.at[g, 1 - keep_a], recv_a.at[g], a_send.at[g], a_recv.at[g], me, bat_a))
@@ -245,7 +250,7 @@
 
     for move in last:
         move.wait_recv()
-    phi_out[...] = fin[...].reshape(slots, own).T
+    phi_out[...] = fin[...].reshape(own, slots)
 
     for g in range(2):
         for at in range(group):
@@ -260,7 +265,6 @@
     rows, width = tokens.shape
     slots = logits.shape[1]
     own = width // n
-    quarter = slots // 4
     scale = float(n * rows // 16)
     dma = pltpu.SemaphoreType.DMA
     hbm = pl.BlockSpec(memory_space=pltpu.HBM)
@@ -282,17 +286,17 @@
             pltpu.VMEM((n, 8, slots), F32),
             pltpu.VMEM((rows, slots), BF16),
             pltpu.VMEM((rows, slots), BF16),
-            pltpu.VMEM((slots, rows), BF16),
-            pltpu.VMEM((2, 2, 2, n // 2, quarter, own), F32),
-            pltpu.VMEM((2, 2, 2, n // 2, quarter, own), BF16),
-            pltpu.VMEM((2, 2, n // 2, quarter, own), BF16),
-            pltpu.VMEM((2, 2, n // 2, quarter, own), F32),
-            pltpu.VMEM((2, 2, n // 2, quarter, own), BF16),
-            pltpu.VMEM((2, n // 2, quarter, own), BF16),
-            pltpu.VMEM((n, quarter, own), F32),
-            pltpu.VMEM((2, n // 2, quarter, own), BF16),
-            pltpu.VMEM((n, quarter, own), BF16),
-            pltpu.VMEM((4, quarter, own), F32),
+            pltpu.VMEM((width, rows), BF16),
+            pltpu.VMEM((2, 2, 2, n // 2, own // 4, slots), F32),
+            pltpu.VMEM((2, 2, 2, n // 2, own // 4, slots), BF16),
+            pltpu.VMEM((2, 2, n // 2, own // 4, slots), BF16),
+            pltpu.VMEM((2, 2, n // 2, own // 4, slots), F32),
+            pltpu.VMEM((2, 2, n // 2, own // 4, slots), BF16),
+            pltpu.VMEM((2, n // 2, own // 4, slots), BF16),
+            pltpu.VMEM((n, own // 4, slots), F32),
+            pltpu.VMEM((2, n // 2, own // 4, slots), BF16),
+            pltpu.VMEM((n, own // 4, slots), BF16),
+            pltpu.VMEM((4, own // 4, slots), F32),
             dma((4,)),
             dma((n // 2, 2)), dma((n // 2, 2)),
             dma((n // 2, 2)), dma((n // 2, 2)),

time: 37.9 us -> 37.6 us (level)
  Pallas kernels: 35.2 us -> 34.8 us
where the time goes in v5:
time: 37.6 us; the launch traced here: 37.4 us
  Pallas kernels  34.8 us (93%)
  local copies, waits for them, and re-layouts  1.98 us (5%)
  between operations  0.64 us (2%)
    pallas_call x1, Pallas kernels, fused(): pl.pallas_call(functools.partial(fused_kernel, n, scale), out_shape=(jax....  34.8 us
    unnamed x2, local copies, waits for them, and re-layouts  1.98 us

profile of v5, /device:TPU:0, one launch (start us, length us, event | category | flops | bytes accessed | tf_op | source)
XLA Modules:
  0.0 37.4 jit_solution(14594746357890213466)
XLA Ops:
  0.6 34.8 %shard_map.59 = (bf16[1024,1024]{1,0:T(8,128)(2,1)S(1)}, f32[128,256]{1,0:T(8,128)S(1)}) custom-call(bf16[1024,1024]{1,0:T(8,128)(2,1)} %bitcast.6, bf16[1024,256]{1,0:T(8,128)(2,1)} %bitcast.7, bf16[32,1024]{1,0:T(8,128)(2,1)} %bitcast.8, bf16[4,32,256]{2,1,0:T(8,128)(2,1)} %bitcast.9), custom_call_target="tpu_custom_call" | custom-call | tf_op jit(solution)/shard_map/pallas_call | solution.py:271
  35.4 1.3 %copy.8 = bf16[1,1024,1024]{2,1,0:T(8,128)(2,1)} copy(bf16[1,1024,1024]{2,1,0:T(8,128)(2,1)S(1)} %bitcast.5) | data formatting | bytes 4194304
  36.8 0.7 %copy.9 = f32[128,256]{1,0:T(8,128)} copy(f32[128,256]{1,0:T(8,128)S(1)} %get-tuple-element.9) | data formatting | bytes 262144
